TPU v7x, 32 devices: a whole 2x2x4 slice. The times are simulated.
32 devices in a mesh: sfc: 8 (over z, core), lev: 4 (over y, x).
Axes of the slice: x: 2, y: 2, z: 4, core: 2. Of those that a mesh axis runs over, the one named last changes fastest.
Arguments:
- tracer_old: float32 [4, 10, 16, 3072], P('lev', None, None, 'sfc'), may hold values from 0.1 to 2
- air_old: float32 [4, 16, 3072], P('lev', None, 'sfc'), may hold values from 0.3 to 20, as said below
- air_new: float32 [4, 16, 3072], P('lev', None, 'sfc'), may hold values from 0.4 to 20, as said below
- dep_coord: float32 [2, 4, 16, 3072], P(None, 'lev', None, 'sfc'), may hold values from -1 to 1
- dep_slot: int32 [4, 16, 3072], P('lev', None, 'sfc'), may hold values from 0 to 639
- fetch_list: int32 [8, 2, 128], P('sfc'), may hold values from 0 to 383, as said below
Outputs:
- tracer_new: float32 [4, 10, 16, 3072], P('lev', None, None, 'sfc')
Inputs may be any that keep to these rules, and one draw needn't show every extreme that they name: `fetch_list`: side 0 holds distinct indices in [128, 384); side 1 holds distinct indices in [0, 256). `air_old`: positive. `air_new`: positive.
All inputs are finite; a program needn't handle non-finite values.
Results may differ from a plain program's by a relative error of at most 0.0003.
Values sent between devices are 32-bit elements; how exact they have to be, the bound alone decides.
A program may use at most 64 MiB of HBM per device.

v0:
```python
import jax
import jax.numpy as jnp
from jax import lax
from jax.sharding import PartitionSpec as P

BAND = 256
NODES = (-1.0, -0.4472135954999579, 0.4472135954999579, 1.0)


def padded(block, sides, width):
    for axis, dim in sides:
        count = lax.axis_size(axis)
        forward = [(i, i + 1) for i in range(count - 1)]
        forward.append((count - 1, 0))
        backward = [(target, source) for source, target in forward]
        low = lax.ppermute(
            lax.slice_in_dim(block, block.shape[dim] - width, None, axis=dim), axis, forward
        )
        high = lax.ppermute(lax.slice_in_dim(block, 0, width, axis=dim), axis, backward)
        block = jnp.concatenate([low, block, high], axis=dim)
    return block


def basis(coord):
    terms = []
    for first in range(4):
        term = jnp.ones_like(coord)
        for other in range(4):
            if other != first:
                term = term * (coord - NODES[other]) / (NODES[first] - NODES[other])
        terms.append(term)
    return terms


def pick_rows(table, slots):
    return table[slots]


def on_device(tracer_old, air_old, air_new, dep_coord, dep_slot, fetch_list):
    e_dev = tracer_old.shape[3]
    levels = tracer_old.shape[0]
    tracers = tracer_old.shape[1]
    points = tracer_old.shape[2]
    old_term = jnp.sum(air_old[:, None] * tracer_old, axis=(0, 2, 3))
    old_mass = lax.psum(old_term, ("sfc", "lev"))
    extended = padded(tracer_old, (("sfc", 3),), BAND)
    left = jnp.take(extended, fetch_list[0, 0] - (e_dev - BAND), axis=3)
    right = jnp.take(extended, BAND + e_dev + fetch_list[0, 1], axis=3)
    buffer = jnp.concatenate([tracer_old, left, right], axis=3)
    width = buffer.shape[3]
    rows = jnp.transpose(buffer, (0, 3, 1, 2)).reshape(levels, width, tracers * points)
    picked = jax.vmap(pick_rows)(rows, dep_slot)
    picked = picked.reshape(levels, points, e_dev, tracers, 16)
    along_a = basis(dep_coord[0])
    along_b = basis(dep_coord[1])
    stacked = jnp.stack([along_a[j // 4] * along_b[j % 4] for j in range(16)], axis=-1)
    interp = jnp.sum(picked * stacked[:, :, :, None, :], axis=-1)
    low = jnp.min(picked, axis=-1)
    high = jnp.max(picked, axis=-1)
    interp = jnp.transpose(interp, (0, 3, 1, 2))
    low = jnp.transpose(low, (0, 3, 1, 2))
    high = jnp.transpose(high, (0, 3, 1, 2))
    clipped = jnp.clip(interp, low, high)
    mass_new = air_new[:, None]
    clip_term = jnp.sum(mass_new * clipped, axis=(0, 2, 3))
    up_term = jnp.sum(mass_new * (high - clipped), axis=(0, 2, 3))
    down_term = jnp.sum(mass_new * (clipped - low), axis=(0, 2, 3))
    summed = lax.psum(jnp.stack([clip_term, up_term, down_term]), ("sfc", "lev"))
    clip_mass = summed[0]
    room_up = summed[1]
    room_down = summed[2]
    shortfall = (old_mass - clip_mass)[None, :, None, None]
    raised = shortfall * (high - clipped) / room_up[None, :, None, None]
    lowered = shortfall * (clipped - low) / room_down[None, :, None, None]
    return clipped + jnp.where(shortfall >= 0, raised, lowered)


def solution(mesh):
    return jax.shard_map(
        on_device,
        mesh=mesh,
        in_specs=(
            P("lev", None, None, "sfc"),
            P("lev", None, "sfc"),
            P("lev", None, "sfc"),
            P(None, "lev", None, "sfc"),
            P("lev", None, "sfc"),
            P("sfc", None, None),
        ),
        out_specs=P("lev", None, None, "sfc"),
        check_vma=False,
    )
```

profile of v0, /device:TPU:0, one launch (start us, length us, event | category | flops | bytes accessed | tf_op | source)
XLA Modules:
  0.0 146.1 jit_solution(4293965998876197416)
XLA Ops:
  0.0 1.0 fusion.7
  1.0 0.5 collective-permute-start
  1.6 4.1 %collective-permute-start.1 = (f32[1,10,16,256]{3,2,1,0:T(8,128)S(1)}, f32[1,10,16,256]{3,2,1,0:T(8,128)S(1)}, u32[]{:S(2)}, u32[]{:S(2)}) collective-permute-start(f32[1,10,16,256]{3,2,1,0:T(8,128)S(1)} %get-tuple-element.22), channel_id=1, source_target_pairs={{4,0},{8,4},{12,8},{16,12},{20,16},{24,20},{28,24},{0,28},{5,1},{9... | collective-permute-start | bytes 491528 | tf_op jit(solution)/shard_map/ppermute | solution.py:19
  5.7 0.8 compare_and_fusion.1
  6.4 0.7 fusion.1
  7.2 0.8 constant_dynamic-update-slice_fusion.15
  8.0 0.8 constant_dynamic-update-slice_fusion.14
  8.8 0.8 constant_dynamic-update-slice_fusion.13
  9.5 0.8 constant_dynamic-update-slice_fusion.12
  10.3 0.8 constant_dynamic-update-slice_fusion.11
  11.1 0.8 constant_dynamic-update-slice_fusion.10
  11.9 0.8 constant_dynamic-update-slice_fusion.9
  12.7 0.8 constant_dynamic-update-slice_fusion.8
  13.4 0.8 constant_dynamic-update-slice_fusion.7
  14.2 0.8 constant_dynamic-update-slice_fusion.6
  15.0 0.8 constant_dynamic-update-slice_fusion.5
  15.8 0.8 constant_dynamic-update-slice_fusion.4
  16.5 0.8 constant_dynamic-update-slice_fusion.3
  17.3 0.8 constant_dynamic-update-slice_fusion.2
  18.1 0.8 constant_dynamic-update-slice_fusion.1
  18.9 0.8 constant_dynamic-update-slice_fusion
  19.7 0.0 copy-start.1
  19.7 0.7 copy-done.1
  20.4 1.1 multiply_reduce_fusion.4
  21.5 0.0 collective-permute-done
  21.5 0.0 collective-permute-done.1
  21.5 1.0 pad_maximum_fusion
  22.5 5.8 %copy.16 = f32[1,10,16,896]{2,1,3,0:T(8,128)} copy(f32[1,10,16,896]{3,2,1,0:T(8,128)S(1)} %pad_maximum_fusion) | data formatting | bytes 1146880 | tf_op jit(solution)/shard_map/concatenate | solution.py:20
  28.4 0.0 copy-start
  28.4 3.8 %gather_fusion.1 = f32[128,10,16]{2,1,0:T(8,128)S(1)} fusion(f32[10,16,896]{1,0,2:T(8,128)} %bitcast.103, s32[1024]{0:T(1024)S(1)} %pad_clamp_fusion.1), kind=kCustom, calls=%fused_computation.clone | custom fusion | bytes 164352 | tf_op jit(solution)/shard_map/jit(_take)/gather | solution.py:47
  32.1 4.7 %gather_fusion.2 = f32[128,10,16]{2,1,0:T(8,128)} fusion(f32[10,16,896]{1,0,2:T(8,128)} %bitcast.104, s32[1024]{0:T(1024)S(1)} %pad_clamp_fusion), kind=kCustom, calls=%fused_computation.1.clone | custom fusion | bytes 164352 | tf_op jit(solution)/shard_map/jit(_take)/gather | solution.py:48
  36.8 1.6 %bitcast_select_fusion = (f32[1,10,16,128]{2,1,3,0:T(8,128)S(1)}, f32[1,10,16,128]{2,1,3,0:T(8,128)S(1)}) fusion(f32[128,10,16]{2,1,0:T(8,128)} %gather_fusion.2, pred[128]{0:T(512)(128)(4,1)S(1)} %get-tuple-element.25, f32[128,10,16]{2,1,0:T(8,128)S(1)} %gather_fusion.1, pred[128]{0:T(512)(128)(4,1)S(1)} %get-tuple-element.17), kind=kLoop, calls=%fused_computation.4 | loop fusion | flops 40960 | bytes 327936 | tf_op jit(solution)/shard_map/jit(_take)/select_n | solution.py:48
  38.4 0.3 copy.18
  38.7 0.3 copy.19
  39.0 0.0 copy-done
  39.0 0.2 copy.20
  39.3 57.0 %gather_fusion = f32[6144,160]{1,0:T(8,128)} fusion(f32[1,640,160]{2,1,0:T(8,128)S(1)} %copy.20, s32[6144]{0:T(1024)S(1)} %reshape.935), kind=kCustom, calls=%fused_computation.2 | custom fusion | bytes 7913472 | tf_op jit(solution)/shard_map/vmap()/gather | solution.py:36
  96.3 6.0 %copy.21 = f32[6144,160]{0,1:T(8,128)} copy(f32[6144,160]{1,0:T(8,128)} %gather_fusion) | data formatting | bytes 7864320 | tf_op jit(solution)/shard_map/vmap()/gather | solution.py:36
  102.2 0.0 copy-start.2
  102.2 2.9 %copy.22 = f32[20,8,16,384]{3,2,1,0:T(8,128)S(1)} copy(f32[20,8,16,384]{3,1,2,0:T(8,128)} %bitcast.102) | data formatting | bytes 7864320
  105.1 0.0 copy-start.3
  105.1 0.0 copy-done.2
  105.1 0.5 fusion.5
  105.7 0.2 copy-done.3
  105.8 0.2 multiply_reduce_fusion.3
  106.1 39.2 %all-reduce = (f32[3,10]{1,0:T(4,128)S(1)}, f32[10]{0:T(128)S(1)}) all-reduce(f32[3,10]{1,0:T(4,128)S(1)} %pad_maximum_fusion.2, f32[10]{0:T(128)S(1)} %multiply_reduce_fusion.4), channel_id=1, replica_groups=mesh['sfc'=8,'lev'=4] {'sfc','lev'}, use_global_device_ids=true, to_apply=%region_8.10 | all-reduce | flops 40 | bytes 320 | tf_op jit(solution)/shard_map/psum | solution.py:68
  145.2 0.9 select_add_fusion
  (9 shorter events, 0.1 us)
Async XLA Ops:
  1.0 20.5 %collective-permute-start = (f32[1,10,16,256]{3,2,1,0:T(8,128)S(1)}, f32[1,10,16,256]{3,2,1,0:T(8,128)S(1)}, u32[]{:S(2)}, u32[]{:S(2)}) collective-permute-start(f32[1,10,16,256]{3,2,1,0:T(8,128)S(1)} %get-tuple-element.21), channel_id=1, source_target_pairs={{0,4},{4,8},{8,12},{12,16},{16,20},{20,24},{24,28},{28,0},{1,5},{5... | collective-permute-start | bytes 491528 | tf_op jit(solution)/shard_map/ppermute | solution.py:16
  1.6 20.0 %collective-permute-start.1 = (f32[1,10,16,256]{3,2,1,0:T(8,128)S(1)}, f32[1,10,16,256]{3,2,1,0:T(8,128)S(1)}, u32[]{:S(2)}, u32[]{:S(2)}) collective-permute-start(f32[1,10,16,256]{3,2,1,0:T(8,128)S(1)} %get-tuple-element.22), channel_id=1, source_target_pairs={{4,0},{8,4},{12,8},{16,12},{20,16},{24,20},{28,24},{0,28},{5,1},{9... | collective-permute-start | bytes 491528 | tf_op jit(solution)/shard_map/ppermute | solution.py:19
  19.7 0.7 copy-start.1
  28.4 10.6 %copy-start = (f32[1,10,16,384]{3,2,1,0:T(8,128)S(1)}, f32[1,10,16,384]{3,2,1,0:T(8,128)}, u32[]{:S(2)}) copy-start(f32[1,10,16,384]{3,2,1,0:T(8,128)} %param.8) | copy-start | bytes 737284
  102.2 2.9 %copy-start.2 = (f32[1,16,384,16]{2,1,3,0:T(8,128)S(1)}, f32[1,16,384,16]{2,1,3,0:T(8,128)}, u32[]{:S(2)}) copy-start(f32[1,16,384,16]{2,1,3,0:T(8,128)} %copy-done.1) | copy-start | bytes 1179652
  105.1 0.7 copy-start.3
where the time goes:
time: 148 us; the launch traced here: 146 us
  local copies, waits for them, and re-layouts  82.9 us (56%)
  blocking collectives  39.2 us (26%)
  other arithmetic  19.3 us (13%)
  starting transfers between devices  4.64 us (3%)
    gather x4, local copies, waits for them, and re-layouts, pick_rows(): return table[slots]  63 us
    psum x1, blocking collectives, on_device(): lax.psum(jnp.stack([clip_term, up_term, down_term]), ('sfc', 'lev'))  39.2 us
    unnamed x15, other arithmetic  11.7 us
    concatenate x1, local copies, waits for them, and re-layouts, padded(): block = jnp.concatenate([low, block, high], axis=dim)  5.84 us
    gather x1, local copies, waits for them, and re-layouts, on_device(): right = jnp.take(extended, BAND + e_dev + fetch_list[0, 1], axis=3)  4.7 us
    ppermute x1, starting transfers between devices, padded(): lax.ppermute(lax.slice_in_dim(block, 0, width, axis=dim), axis, backward)  4.09 us
    unnamed x9, local copies, waits for them, and re-layouts  3.77 us
    gather x1, local copies, waits for them, and re-layouts, on_device(): left = jnp.take(extended, fetch_list[0, 0] - (e_dev - BAND), axis=3)  3.77 us
  transfers between devices with their start and end apart: 2, of which 0 were waited for; matrix products, arithmetic and copies ran while one was open for 10% of the time, Pallas kernels for 0%

commit v1 on v0

--- a/solution.py
+++ b/solution.py
@@ -65,7 +65,7 @@
     clip_term = jnp.sum(mass_new * clipped, axis=(0, 2, 3))
     up_term = jnp.sum(mass_new * (high - clipped), axis=(0, 2, 3))
     down_term = jnp.sum(mass_new * (clipped - low), axis=(0, 2, 3))
-    summed = lax.psum(jnp.stack([clip_term, up_term, down_term]), ("sfc", "lev"))
+    summed = lax.psum(lax.psum(jnp.stack([clip_term, up_term, down_term]), "lev"), "sfc")
     clip_mass = summed[0]
     room_up = summed[1]
     room_down = summed[2]

time: 148 us -> 181 us (1.22)
  blocking collectives: 39.2 us -> 62.5 us
  other arithmetic: 19.3 us -> 30 us
    psum x1 -> x3, blocking collectives: 39.2 us -> 62.5 us  [the longest x1 39.2 us: on_device(): old_mass = lax.psum(old_term, ('sfc', 'lev'))]
    unnamed x15, other arithmetic: 11.7 us -> 20.7 us
    unnamed x9 -> x5, local copies, waits for them, and re-layouts: 3.77 us -> 2.81 us
  transfers between devices with their start and end apart: 2 -> 2, of which waited for: 0 -> 0; matrix products, arithmetic and copies ran while one was open for 10% -> 14% of each run, Pallas kernels for 0% -> 0%
where the time goes in v1:
time: 181 us; the launch traced here: 179 us
  local copies, waits for them, and re-layouts  81.9 us (45%)
  blocking collectives  62.5 us (35%)
  other arithmetic  30 us (17%)
  starting transfers between devices  4.64 us (3%)
    gather x4, local copies, waits for them, and re-layouts, pick_rows(): return table[slots]  63 us
    psum x1, blocking collectives, on_device(): old_mass = lax.psum(old_term, ('sfc', 'lev'))  39.2 us
    unnamed x15, other arithmetic  20.7 us
    psum x1, blocking collectives, on_device(): lax.psum(lax.psum(jnp.stack([clip_term, up_term, down_term]), 'lev'), 'sfc')  13.6 us
    psum x1, blocking collectives, on_device(): lax.psum(jnp.stack([clip_term, up_term, down_term]), 'lev')  9.74 us
    concatenate x1, local copies, waits for them, and re-layouts, padded(): block = jnp.concatenate([low, block, high], axis=dim)  5.84 us
    gather x1, local copies, waits for them, and re-layouts, on_device(): right = jnp.take(extended, BAND + e_dev + fetch_list[0, 1], axis=3)  4.7 us
    ppermute x1, starting transfers between devices, padded(): lax.ppermute(lax.slice_in_dim(block, 0, width, axis=dim), axis, backward)  4.09 us
  transfers between devices with their start and end apart: 2, of which 0 were waited for; matrix products, arithmetic and copies ran while one was open for 14% of the time, Pallas kernels for 0%

profile of v1, /device:TPU:0, one launch (start us, length us, event | category | flops | bytes accessed | tf_op | source)
XLA Modules:
  0.0 179.1 jit_solution(1257627007938516442)
XLA Ops:
  0.0 1.0 fusion.7
  1.0 0.5 collective-permute-start
  1.6 4.1 %collective-permute-start.1 = (f32[1,10,16,256]{3,2,1,0:T(8,128)S(1)}, f32[1,10,16,256]{3,2,1,0:T(8,128)S(1)}, u32[]{:S(2)}, u32[]{:S(2)}) collective-permute-start(f32[1,10,16,256]{3,2,1,0:T(8,128)S(1)} %get-tuple-element.20), channel_id=1, source_target_pairs={{4,0},{8,4},{12,8},{16,12},{20,16},{24,20},{28,24},{0,28},{5,1},{9... | collective-permute-start | bytes 491528 | tf_op jit(solution)/shard_map/ppermute | solution.py:19
  5.7 0.8 compare_and_fusion.1
  6.4 0.7 fusion.1
  7.2 1.4 constant_dynamic-update-slice_fusion.15
  8.6 1.4 constant_dynamic-update-slice_fusion.14
  9.9 1.4 constant_dynamic-update-slice_fusion.13
  11.3 1.4 constant_dynamic-update-slice_fusion.12
  12.7 1.4 constant_dynamic-update-slice_fusion.11
  14.1 1.4 constant_dynamic-update-slice_fusion.10
  15.5 1.4 constant_dynamic-update-slice_fusion.9
  16.9 1.4 constant_dynamic-update-slice_fusion.8
  18.2 1.4 constant_dynamic-update-slice_fusion.7
  19.6 1.4 constant_dynamic-update-slice_fusion.6
  21.0 1.4 constant_dynamic-update-slice_fusion.5
  22.4 1.4 constant_dynamic-update-slice_fusion.4
  23.7 1.4 constant_dynamic-update-slice_fusion.3
  25.1 1.4 constant_dynamic-update-slice_fusion.2
  26.5 1.4 constant_dynamic-update-slice_fusion.1
  27.9 1.4 constant_dynamic-update-slice_fusion
  29.2 1.1 multiply_reduce_fusion.4
  30.3 39.2 %psum.21 = f32[10]{0:T(128)S(1)} all-reduce(f32[10]{0:T(128)S(1)} %multiply_reduce_fusion.4), channel_id=1, replica_groups=mesh['sfc'=8,'lev'=4] {'sfc','lev'}, use_global_device_ids=true, to_apply=%region_4.6 | all-reduce | flops 10 | bytes 80 | tf_op jit(solution)/shard_map/psum | solution.py:45
  69.5 0.0 collective-permute-done
  69.5 0.0 collective-permute-done.1
  69.5 1.0 pad_maximum_fusion
  70.5 5.8 %copy.16 = f32[1,10,16,896]{2,1,3,0:T(8,128)} copy(f32[1,10,16,896]{3,2,1,0:T(8,128)S(1)} %pad_maximum_fusion) | data formatting | bytes 1146880 | tf_op jit(solution)/shard_map/concatenate | solution.py:20
  76.4 0.0 copy-start
  76.4 3.8 %gather_fusion.1 = f32[128,10,16]{2,1,0:T(8,128)S(1)} fusion(f32[10,16,896]{1,0,2:T(8,128)} %bitcast.103, s32[1024]{0:T(1024)S(1)} %pad_clamp_fusion.1), kind=kCustom, calls=%fused_computation.clone | custom fusion | bytes 164352 | tf_op jit(solution)/shard_map/jit(_take)/gather | solution.py:47
  80.1 4.7 %gather_fusion.2 = f32[128,10,16]{2,1,0:T(8,128)} fusion(f32[10,16,896]{1,0,2:T(8,128)} %bitcast.104, s32[1024]{0:T(1024)S(1)} %pad_clamp_fusion), kind=kCustom, calls=%fused_computation.1.clone | custom fusion | bytes 164352 | tf_op jit(solution)/shard_map/jit(_take)/gather | solution.py:48
  84.9 1.6 bitcast_select_fusion
  86.4 0.3 copy.18
  86.7 0.3 copy.19
  87.0 0.0 copy-done
  87.0 0.2 copy.20
  87.3 57.0 %gather_fusion = f32[6144,160]{1,0:T(8,128)} fusion(f32[1,640,160]{2,1,0:T(8,128)S(1)} %copy.20, s32[6144]{0:T(1024)S(1)} %reshape.935), kind=kCustom, calls=%fused_computation.2 | custom fusion | bytes 7913472 | tf_op jit(solution)/shard_map/vmap()/gather | solution.py:36
  144.3 6.0 %copy.21 = f32[6144,160]{0,1:T(8,128)} copy(f32[6144,160]{1,0:T(8,128)} %gather_fusion) | data formatting | bytes 7864320 | tf_op jit(solution)/shard_map/vmap()/gather | solution.py:36
  150.3 2.8 %copy.22 = f32[20,8,16,384]{3,2,1,0:T(8,128)S(1)} copy(f32[20,8,16,384]{3,1,2,0:T(8,128)} %bitcast.102) | data formatting | bytes 7864320
  153.1 0.0 copy-start.1
  153.1 1.6 fusion.5
  154.7 0.0 copy-done.1
  154.7 0.2 multiply_reduce_fusion.3
  154.9 9.7 %psum.22 = f32[3,10]{1,0:T(4,128)S(1)} all-reduce(f32[3,10]{1,0:T(4,128)S(1)} %pad_maximum_fusion.2), channel_id=1, replica_groups=mesh['sfc'=8,'lev'=4] {'lev'}, use_global_device_ids=true, to_apply=%region_8.10 | all-reduce | flops 30 | bytes 240 | tf_op jit(solution)/shard_map/psum | solution.py:68
  164.7 13.6 %psum.23 = f32[3,10]{1,0:T(4,128)S(1)} all-reduce(f32[3,10]{1,0:T(4,128)S(1)} %psum.22), channel_id=1, replica_groups=mesh['sfc'=8,'lev'=4] {'sfc'}, use_global_device_ids=true, to_apply=%region_9.11 | all-reduce | flops 30 | bytes 240 | tf_op jit(solution)/shard_map/psum | solution.py:68
  178.3 0.9 select_add_fusion
  (9 shorter events, 0.1 us)
Async XLA Ops:
  1.0 68.5 %collective-permute-start = (f32[1,10,16,256]{3,2,1,0:T(8,128)S(1)}, f32[1,10,16,256]{3,2,1,0:T(8,128)S(1)}, u32[]{:S(2)}, u32[]{:S(2)}) collective-permute-start(f32[1,10,16,256]{3,2,1,0:T(8,128)S(1)} %get-tuple-element.19), channel_id=1, source_target_pairs={{0,4},{4,8},{8,12},{12,16},{16,20},{20,24},{24,28},{28,0},{1,5},{5... | collective-permute-start | bytes 491528 | tf_op jit(solution)/shard_map/ppermute | solution.py:16
  1.6 68.0 %collective-permute-start.1 = (f32[1,10,16,256]{3,2,1,0:T(8,128)S(1)}, f32[1,10,16,256]{3,2,1,0:T(8,128)S(1)}, u32[]{:S(2)}, u32[]{:S(2)}) collective-permute-start(f32[1,10,16,256]{3,2,1,0:T(8,128)S(1)} %get-tuple-element.20), channel_id=1, source_target_pairs={{4,0},{8,4},{12,8},{16,12},{20,16},{24,20},{28,24},{0,28},{5,1},{9... | collective-permute-start | bytes 491528 | tf_op jit(solution)/shard_map/ppermute | solution.py:19
  76.4 10.6 %copy-start = (f32[1,10,16,384]{3,2,1,0:T(8,128)S(1)}, f32[1,10,16,384]{3,2,1,0:T(8,128)}, u32[]{:S(2)}) copy-start(f32[1,10,16,384]{3,2,1,0:T(8,128)} %param.8) | copy-start | bytes 737284
  153.1 1.6 copy-start.1

commit v2 on v0

--- a/solution.py
+++ b/solution.py
@@ -65,7 +65,9 @@
     clip_term = jnp.sum(mass_new * clipped, axis=(0, 2, 3))
     up_term = jnp.sum(mass_new * (high - clipped), axis=(0, 2, 3))
     down_term = jnp.sum(mass_new * (clipped - low), axis=(0, 2, 3))
-    summed = lax.psum(jnp.stack([clip_term, up_term, down_term]), ("sfc", "lev"))
+    summed = jnp.sum(
+        lax.all_gather(jnp.stack([clip_term, up_term, down_term]), ("sfc", "lev")), axis=0
+    )
     clip_mass = summed[0]
     room_up = summed[1]
     room_down = summed[2]

time: 148 us -> 224 us (1.51)
  blocking collectives: 39.2 us -> 105 us
  other arithmetic: 19.3 us -> 30 us
    all_gather x0 -> x1, blocking collectives: none -> 66.2 us  [on_device(): lax.all_gather(jnp.stack([clip_term, up_term, down_term]), ('sfc', 'lev'))]
    unnamed x15 -> x16, other arithmetic: 11.7 us -> 20.7 us
  transfers between devices with their start and end apart: 2 -> 2, of which waited for: 0 -> 0; matrix products, arithmetic and copies ran while one was open for 10% -> 11% of each run, Pallas kernels for 0% -> 0%
where the time goes in v2:
time: 224 us; the launch traced here: 222 us
  blocking collectives  105 us (47%)
  local copies, waits for them, and re-layouts  81.9 us (37%)
  other arithmetic  30 us (13%)
  starting transfers between devices  4.64 us (2%)
    all_gather x1, blocking collectives, on_device(): lax.all_gather(jnp.stack([clip_term, up_term, down_term]), ('sfc', 'lev'))  66.2 us
    gather x4, local copies, waits for them, and re-layouts, pick_rows(): return table[slots]  63 us
    psum x1, blocking collectives, on_device(): old_mass = lax.psum(old_term, ('sfc', 'lev'))  39.2 us
    unnamed x16, other arithmetic  20.7 us
    concatenate x1, local copies, waits for them, and re-layouts, padded(): block = jnp.concatenate([low, block, high], axis=dim)  5.84 us
    gather x1, local copies, waits for them, and re-layouts, on_device(): right = jnp.take(extended, BAND + e_dev + fetch_list[0, 1], axis=3)  4.7 us
  transfers between devices with their start and end apart: 2, of which 0 were waited for; matrix products, arithmetic and copies ran while one was open for 11% of the time, Pallas kernels for 0%

profile of v2, /device:TPU:0, one launch (start us, length us, event | category | flops | bytes accessed | tf_op | source)
XLA Modules:
  0.0 222.0 jit_solution(14577949967915466645)
XLA Ops:
  0.0 1.0 fusion.7
  1.0 0.5 collective-permute-start
  1.6 4.1 %collective-permute-start.1 = (f32[1,10,16,256]{3,2,1,0:T(8,128)S(1)}, f32[1,10,16,256]{3,2,1,0:T(8,128)S(1)}, u32[]{:S(2)}, u32[]{:S(2)}) collective-permute-start(f32[1,10,16,256]{3,2,1,0:T(8,128)S(1)} %get-tuple-element.20), channel_id=1, source_target_pairs={{4,0},{8,4},{12,8},{16,12},{20,16},{24,20},{28,24},{0,28},{5,1},{9... | collective-permute-start | bytes 491528 | tf_op jit(solution)/shard_map/ppermute | solution.py:19
  5.7 0.8 compare_and_fusion.1
  6.4 0.7 fusion.1
  7.2 1.4 constant_dynamic-update-slice_fusion.15
  8.6 1.4 constant_dynamic-update-slice_fusion.14
  9.9 1.4 constant_dynamic-update-slice_fusion.13
  11.3 1.4 constant_dynamic-update-slice_fusion.12
  12.7 1.4 constant_dynamic-update-slice_fusion.11
  14.1 1.4 constant_dynamic-update-slice_fusion.10
  15.5 1.4 constant_dynamic-update-slice_fusion.9
  16.9 1.4 constant_dynamic-update-slice_fusion.8
  18.2 1.4 constant_dynamic-update-slice_fusion.7
  19.6 1.4 constant_dynamic-update-slice_fusion.6
  21.0 1.4 constant_dynamic-update-slice_fusion.5
  22.4 1.4 constant_dynamic-update-slice_fusion.4
  23.7 1.4 constant_dynamic-update-slice_fusion.3
  25.1 1.4 constant_dynamic-update-slice_fusion.2
  26.5 1.4 constant_dynamic-update-slice_fusion.1
  27.9 1.4 constant_dynamic-update-slice_fusion
  29.2 1.1 multiply_reduce_fusion.4
  30.3 39.2 %psum.7 = f32[10]{0:T(128)S(1)} all-reduce(f32[10]{0:T(128)S(1)} %multiply_reduce_fusion.4), channel_id=1, replica_groups=mesh['sfc'=8,'lev'=4] {'sfc','lev'}, use_global_device_ids=true, to_apply=%region_4.6 | all-reduce | flops 10 | bytes 80 | tf_op jit(solution)/shard_map/psum | solution.py:45
  69.5 0.0 collective-permute-done
  69.5 0.0 collective-permute-done.1
  69.5 1.0 pad_maximum_fusion
  70.5 5.8 %copy.16 = f32[1,10,16,896]{2,1,3,0:T(8,128)} copy(f32[1,10,16,896]{3,2,1,0:T(8,128)S(1)} %pad_maximum_fusion) | data formatting | bytes 1146880 | tf_op jit(solution)/shard_map/concatenate | solution.py:20
  76.4 0.0 copy-start
  76.4 3.8 %gather_fusion.1 = f32[128,10,16]{2,1,0:T(8,128)S(1)} fusion(f32[10,16,896]{1,0,2:T(8,128)} %bitcast.105, s32[1024]{0:T(1024)S(1)} %pad_clamp_fusion.1), kind=kCustom, calls=%fused_computation.clone | custom fusion | bytes 164352 | tf_op jit(solution)/shard_map/jit(_take)/gather | solution.py:47
  80.1 4.7 %gather_fusion.2 = f32[128,10,16]{2,1,0:T(8,128)} fusion(f32[10,16,896]{1,0,2:T(8,128)} %bitcast.106, s32[1024]{0:T(1024)S(1)} %pad_clamp_fusion), kind=kCustom, calls=%fused_computation.1.clone | custom fusion | bytes 164352 | tf_op jit(solution)/shard_map/jit(_take)/gather | solution.py:48
  84.9 1.6 bitcast_select_fusion
  86.4 0.3 copy.18
  86.7 0.3 copy.19
  87.0 0.0 copy-done
  87.0 0.2 copy.20
  87.3 57.0 %gather_fusion = f32[6144,160]{1,0:T(8,128)} fusion(f32[1,640,160]{2,1,0:T(8,128)S(1)} %copy.20, s32[6144]{0:T(1024)S(1)} %reshape.935), kind=kCustom, calls=%fused_computation.2 | custom fusion | bytes 7913472 | tf_op jit(solution)/shard_map/vmap()/gather | solution.py:36
  144.3 6.0 %copy.21 = f32[6144,160]{0,1:T(8,128)} copy(f32[6144,160]{1,0:T(8,128)} %gather_fusion) | data formatting | bytes 7864320 | tf_op jit(solution)/shard_map/vmap()/gather | solution.py:36
  150.3 2.8 %copy.22 = f32[20,8,16,384]{3,2,1,0:T(8,128)S(1)} copy(f32[20,8,16,384]{3,1,2,0:T(8,128)} %bitcast.104) | data formatting | bytes 7864320
  153.1 0.0 copy-start.1
  153.1 1.6 fusion.5
  154.7 0.0 copy-done.1
  154.7 0.2 multiply_reduce_fusion.3
  154.9 66.2 %all-gather.1 = f32[32,3,10]{2,1,0:T(4,128)S(1)} all-gather(f32[1,3,10]{2,1,0:T(4,128)S(1)} %maximum_bitcast_fusion), channel_id=2, replica_groups=mesh['sfc'=8,'lev'=4] {'sfc','lev'}, dimensions={0}, use_global_device_ids=true | all-gather | bytes 3960 | tf_op jit(solution)/shard_map/all_gather | solution.py:69
  221.2 0.9 select_add_fusion
  (10 shorter events, 0.1 us)
Async XLA Ops:
  1.0 68.5 %collective-permute-start = (f32[1,10,16,256]{3,2,1,0:T(8,128)S(1)}, f32[1,10,16,256]{3,2,1,0:T(8,128)S(1)}, u32[]{:S(2)}, u32[]{:S(2)}) collective-permute-start(f32[1,10,16,256]{3,2,1,0:T(8,128)S(1)} %get-tuple-element.19), channel_id=1, source_target_pairs={{0,4},{4,8},{8,12},{12,16},{16,20},{20,24},{24,28},{28,0},{1,5},{5... | collective-permute-start | bytes 491528 | tf_op jit(solution)/shard_map/ppermute | solution.py:16
  1.6 68.0 %collective-permute-start.1 = (f32[1,10,16,256]{3,2,1,0:T(8,128)S(1)}, f32[1,10,16,256]{3,2,1,0:T(8,128)S(1)}, u32[]{:S(2)}, u32[]{:S(2)}) collective-permute-start(f32[1,10,16,256]{3,2,1,0:T(8,128)S(1)} %get-tuple-element.20), channel_id=1, source_target_pairs={{4,0},{8,4},{12,8},{16,12},{20,16},{24,20},{28,24},{0,28},{5,1},{9... | collective-permute-start | bytes 491528 | tf_op jit(solution)/shard_map/ppermute | solution.py:19
  76.4 10.6 %copy-start = (f32[1,10,16,384]{3,2,1,0:T(8,128)S(1)}, f32[1,10,16,384]{3,2,1,0:T(8,128)}, u32[]{:S(2)}) copy-start(f32[1,10,16,384]{3,2,1,0:T(8,128)} %param.8) | copy-start | bytes 737284
  153.1 1.6 copy-start.1
